TPU v7x, 32 devices: a whole 2x2x4 slice. The times are simulated.
32 devices in a mesh: shard: 4 (over z), replica: 8 (over y, x, core).
Axes of the slice: x: 2, y: 2, z: 4, core: 2. Of those that a mesh axis runs over, the one named last changes fastest.
Arguments:
- block_in: bfloat16 [4096, 2048], P(('shard', 'replica')), may hold values from -6 to 6
- positions: int32 [4096], P(('shard', 'replica')), may hold values from 0 to 127, as said below
- out_grad: bfloat16 [4096, 2048], P(('shard', 'replica')), may hold values from -6 to 6
- w_qkv: bfloat16 [2048, 6144], P('shard'), may hold values from -0.125 to 0.125
- b_qkv: bfloat16 [6144], P('shard'), may hold values from -4.75 to 4.75
- w_out: bfloat16 [2048, 2048], P('shard'), may hold values from -0.25 to 0.25
- b_out: bfloat16 [2048], P('shard'), may hold values from -3 to 3
- w_up: bfloat16 [2048, 8192], P('shard'), may hold values from -0.125 to 0.125
- b_up: bfloat16 [8192], P('shard'), may hold values from -3 to 3
- w_down: bfloat16 [8192, 2048], P('shard'), may hold values from -0.0625 to 0.0625
- b_down: bfloat16 [2048], P('shard'), may hold values from -3 to 3
- first_gain: bfloat16 [2048], P('shard'), may hold values from 0.5 to 1.5
- first_shift: bfloat16 [2048], P('shard'), may hold values from -3 to 3
- second_gain: bfloat16 [2048], P('shard'), may hold values from 0.5 to 1.5
- second_shift: bfloat16 [2048], P('shard'), may hold values from -3 to 3
Outputs:
- block_out: bfloat16 [4096, 2048], P(('shard', 'replica'))
- in_grad: bfloat16 [4096, 2048], P(('shard', 'replica'))
- grad_w_qkv: float32 [2048, 6144], P('shard')
- grad_b_qkv: float32 [6144], P('shard')
- grad_w_out: float32 [2048, 2048], P('shard')
- grad_b_out: float32 [2048], P('shard')
- grad_w_up: float32 [2048, 8192], P('shard')
- grad_b_up: float32 [8192], P('shard')
- grad_w_down: float32 [8192, 2048], P('shard')
- grad_b_down: float32 [2048], P('shard')
- grad_first_gain: float32 [2048], P('shard')
- grad_first_shift: float32 [2048], P('shard')
- grad_second_gain: float32 [2048], P('shard')
- grad_second_shift: float32 [2048], P('shard')
Inputs may be any that keep to these rules, and one draw needn't show every extreme that they name: `positions`: each device's 128 tokens hold whole sequences: a position is 0 at a sequence's start and at each device's first token and otherwise one more than the position before; some device holds one sequence of 128 tokens.
All inputs are finite; a program needn't handle non-finite values.
Results may differ from a plain program's by a relative error of at most 0.006.
The roundings to bfloat16 on the way count: a program that leaves them out, or rounds other values in their place, can miss the bound.
Values may be sent and summed in bfloat16 or wider, within the bound.
A program may use at most 384 MiB of HBM per device.

v0:
```python
import jax
import jax.numpy as jnp
from jax import lax
from jax.sharding import PartitionSpec as P

D = 2048
H = 8
HD = 256
ROT = 64
epsilon = 1e-05


def norm_forward(values, gain, shift):
    centre = jnp.mean(values, axis=-1, keepdims=True)
    offsets = values - centre
    spread = jnp.mean(offsets * offsets, axis=-1, keepdims=True)
    inverse = lax.rsqrt(spread + epsilon)
    normed = offsets * inverse
    return (normed * gain.astype(jnp.float32) + shift.astype(jnp.float32), normed, inverse)


def norm_backward(upstream, normed, inverse, gain):
    scaled = upstream * gain.astype(jnp.float32)
    inward = inverse * (
        scaled
        - jnp.mean(scaled, axis=-1, keepdims=True)
        - normed * jnp.mean(scaled * normed, axis=-1, keepdims=True)
    )
    return (inward, jnp.sum(upstream * normed, axis=0), jnp.sum(upstream, axis=0))


def rotary_tables(positions):
    half_rot = ROT // 2
    freqs = 10000.0 ** (-(jnp.arange(half_rot, dtype=jnp.float32) * (2.0 / ROT)))
    angles = positions.astype(jnp.float32)[:, None] * freqs[None, :]
    return (jnp.cos(angles)[:, None, :], jnp.sin(angles)[:, None, :])


def rotate(values, cosine, sine):
    half_rot = ROT // 2
    first = values[..., :half_rot]
    second = values[..., half_rot:ROT]
    return jnp.concatenate(
        [first * cosine - second * sine, second * cosine + first * sine, values[..., ROT:]], axis=-1
    )


def gelu_value(values):
    return 0.5 * values * (1.0 + lax.erf(values * 0.7071067811865476))


def gelu_slope(values):
    return (
        0.5 * (1.0 + lax.erf(values * 0.7071067811865476))
        + values * jnp.exp(-0.5 * values * values) * 0.3989422804014327
    )


def contract_rows(left, right):
    return lax.dot_general(
        left, right, (((0,), (0,)), ((), ())), preferred_element_type=jnp.float32
    )


def times_transpose(left, right):
    return lax.dot_general(
        left, right, (((1,), (1,)), ((), ())), preferred_element_type=jnp.float32
    )


def causal_mask(positions):
    count = positions.shape[0]
    index = jnp.arange(count, dtype=jnp.int32)
    behind = index[:, None] - index[None, :]
    return (behind >= 0) & (behind <= positions[:, None])


def attend_forward(queries, keys, values, positions):
    allowed = causal_mask(positions)[None]
    scale = HD ** (-0.5)
    scores = jnp.einsum("qhd,khd->hqk", queries, keys, preferred_element_type=jnp.float32) * scale
    scores = jnp.where(allowed, scores, -1e30)
    peak = jnp.max(scores, axis=-1, keepdims=True)
    logsum = peak + jnp.log(jnp.sum(jnp.exp(scores - peak), axis=-1, keepdims=True))
    probs = jnp.exp(scores - logsum).astype(jnp.bfloat16)
    outputs = jnp.einsum("hqk,khd->qhd", probs, values, preferred_element_type=jnp.float32).astype(
        jnp.bfloat16
    )
    return (outputs.reshape(queries.shape[0], D), logsum[..., 0])


def attend_backward(queries, keys, values, attended_grad, logsums, positions):
    allowed = causal_mask(positions)[None]
    scale = HD ** (-0.5)
    upstream = attended_grad.reshape(queries.shape[0], H, HD)
    scores = jnp.einsum("qhd,khd->hqk", queries, keys, preferred_element_type=jnp.float32) * scale
    scores = jnp.where(allowed, scores, -1e30)
    probs = jnp.exp(scores - logsums[..., None])
    probs_low = probs.astype(jnp.bfloat16)
    dprobs = jnp.einsum("qhd,khd->hqk", upstream, values, preferred_element_type=jnp.float32)
    total = jnp.sum(probs * dprobs, axis=-1, keepdims=True)
    dscores = (probs * (dprobs - total) * scale).astype(jnp.bfloat16)
    query_grad = jnp.einsum("hqk,khd->qhd", dscores, keys, preferred_element_type=jnp.float32)
    key_grad = jnp.einsum("hqk,qhd->khd", dscores, queries, preferred_element_type=jnp.float32)
    value_grad = jnp.einsum("hqk,qhd->khd", probs_low, upstream, preferred_element_type=jnp.float32)
    return (query_grad, key_grad, value_grad)


def layer_forward(block_in, positions, params):
    (
        w_qkv,
        b_qkv,
        w_out,
        b_out,
        w_up,
        b_up,
        w_down,
        b_down,
        first_gain,
        first_shift,
        second_gain,
        second_shift,
    ) = params
    count = block_in.shape[0]
    wide_in = block_in.astype(jnp.float32)
    first_full, first_normed, first_inverse = norm_forward(wide_in, first_gain, first_shift)
    second_full, second_normed, second_inverse = norm_forward(wide_in, second_gain, second_shift)
    first_low = first_full.astype(jnp.bfloat16)
    second_low = second_full.astype(jnp.bfloat16)
    mixed = jnp.dot(first_low, w_qkv, preferred_element_type=jnp.float32) + b_qkv.astype(
        jnp.float32
    )
    cosine, sine = rotary_tables(positions)
    queries = rotate(mixed[:, :D].reshape(count, H, HD), cosine, sine).astype(jnp.bfloat16)
    keys = rotate(mixed[:, D : 2 * D].reshape(count, H, HD), cosine, sine).astype(jnp.bfloat16)
    values = mixed[:, 2 * D :].reshape(count, H, HD).astype(jnp.bfloat16)
    attended, logsums = attend_forward(queries, keys, values, positions)
    branch_attn = jnp.dot(attended, w_out, preferred_element_type=jnp.float32) + b_out.astype(
        jnp.float32
    )
    hidden_pre = jnp.dot(second_low, w_up, preferred_element_type=jnp.float32) + b_up.astype(
        jnp.float32
    )
    activated = gelu_value(hidden_pre).astype(jnp.bfloat16)
    branch_ffn = jnp.dot(activated, w_down, preferred_element_type=jnp.float32) + b_down.astype(
        jnp.float32
    )
    block_out = (wide_in + branch_attn + branch_ffn).astype(jnp.bfloat16)
    saved = (
        first_normed,
        first_inverse,
        second_normed,
        second_inverse,
        first_low,
        second_low,
        queries,
        keys,
        values,
        attended,
        logsums,
        hidden_pre,
        activated,
        cosine,
        sine,
        positions,
    )
    return (block_out, saved)


def layer_backward(saved, out_grad, params):
    (
        w_qkv,
        b_qkv,
        w_out,
        b_out,
        w_up,
        b_up,
        w_down,
        b_down,
        first_gain,
        first_shift,
        second_gain,
        second_shift,
    ) = params
    (
        first_normed,
        first_inverse,
        second_normed,
        second_inverse,
        first_low,
        second_low,
        queries,
        keys,
        values,
        attended,
        logsums,
        hidden_pre,
        activated,
        cosine,
        sine,
        positions,
    ) = saved
    count = out_grad.shape[0]
    upstream = out_grad.astype(jnp.float32)
    output_sum = jnp.sum(upstream, axis=0)
    hidden_grad = times_transpose(out_grad, w_down) * gelu_slope(hidden_pre)
    grad_b_up = jnp.sum(hidden_grad, axis=0)
    hidden_low = hidden_grad.astype(jnp.bfloat16)
    second_grad = times_transpose(hidden_low, w_up)
    attended_grad = times_transpose(out_grad, w_out).astype(jnp.bfloat16)
    query_grad, key_grad, value_grad = attend_backward(
        queries, keys, values, attended_grad, logsums, positions
    )
    query_grad = rotate(query_grad, cosine, -sine)
    key_grad = rotate(key_grad, cosine, -sine)
    mixed_grad = jnp.concatenate(
        [query_grad.reshape(count, D), key_grad.reshape(count, D), value_grad.reshape(count, D)],
        axis=1,
    )
    grad_b_qkv = jnp.sum(mixed_grad, axis=0)
    mixed_low = mixed_grad.astype(jnp.bfloat16)
    first_grad = times_transpose(mixed_low, w_qkv)
    first_term, grad_first_gain, grad_first_shift = norm_backward(
        first_grad, first_normed, first_inverse, first_gain
    )
    second_term, grad_second_gain, grad_second_shift = norm_backward(
        second_grad, second_normed, second_inverse, second_gain
    )
    in_grad = (upstream + first_term + second_term).astype(jnp.bfloat16)
    small = (
        grad_b_qkv,
        output_sum,
        grad_b_up,
        output_sum,
        grad_first_gain,
        grad_first_shift,
        grad_second_gain,
        grad_second_shift,
    )
    operands = (first_low, mixed_low, attended, second_low, hidden_low, activated)
    return (in_grad, small, operands)


def body(
    block_in,
    positions,
    out_grad,
    w_qkv,
    b_qkv,
    w_out,
    b_out,
    w_up,
    b_up,
    w_down,
    b_down,
    first_gain,
    first_shift,
    second_gain,
    second_shift,
):
    gathered = (
        lax.all_gather(w_qkv, "shard", axis=0, tiled=True),
        lax.all_gather(b_qkv, "shard", axis=0, tiled=True),
        lax.all_gather(w_out, "shard", axis=0, tiled=True),
        lax.all_gather(b_out, "shard", axis=0, tiled=True),
        lax.all_gather(w_up, "shard", axis=0, tiled=True),
        lax.all_gather(b_up, "shard", axis=0, tiled=True),
        lax.all_gather(w_down, "shard", axis=0, tiled=True),
        lax.all_gather(b_down, "shard", axis=0, tiled=True),
        lax.all_gather(first_gain, "shard", axis=0, tiled=True),
        lax.all_gather(first_shift, "shard", axis=0, tiled=True),
        lax.all_gather(second_gain, "shard", axis=0, tiled=True),
        lax.all_gather(second_shift, "shard", axis=0, tiled=True),
    )
    block_out, saved = layer_forward(block_in, positions, gathered)
    regathered = (
        lax.all_gather(w_qkv, "shard", axis=0, tiled=True),
        lax.all_gather(b_qkv, "shard", axis=0, tiled=True),
        lax.all_gather(w_out, "shard", axis=0, tiled=True),
        lax.all_gather(b_out, "shard", axis=0, tiled=True),
        lax.all_gather(w_up, "shard", axis=0, tiled=True),
        lax.all_gather(b_up, "shard", axis=0, tiled=True),
        lax.all_gather(w_down, "shard", axis=0, tiled=True),
        lax.all_gather(b_down, "shard", axis=0, tiled=True),
        lax.all_gather(first_gain, "shard", axis=0, tiled=True),
        lax.all_gather(first_shift, "shard", axis=0, tiled=True),
        lax.all_gather(second_gain, "shard", axis=0, tiled=True),
        lax.all_gather(second_shift, "shard", axis=0, tiled=True),
    )
    in_grad, small, operands = layer_backward(saved, out_grad, regathered)
    first_low, mixed_low, attended, second_low, hidden_low, activated = operands
    full_rows = (
        lax.all_gather(mixed_low, "shard", axis=0, tiled=True),
        lax.all_gather(out_grad, "shard", axis=0, tiled=True),
        lax.all_gather(hidden_low, "shard", axis=0, tiled=True),
    )
    own_columns = (
        lax.all_to_all(first_low, "shard", split_axis=1, concat_axis=0, tiled=True),
        lax.all_to_all(attended, "shard", split_axis=1, concat_axis=0, tiled=True),
        lax.all_to_all(second_low, "shard", split_axis=1, concat_axis=0, tiled=True),
        lax.all_to_all(activated, "shard", split_axis=1, concat_axis=0, tiled=True),
    )
    owned_small = (
        lax.psum_scatter(small[0], "shard", scatter_dimension=0, tiled=True),
        lax.psum_scatter(small[1], "shard", scatter_dimension=0, tiled=True),
        lax.psum_scatter(small[2], "shard", scatter_dimension=0, tiled=True),
        lax.psum_scatter(small[3], "shard", scatter_dimension=0, tiled=True),
        lax.psum_scatter(small[4], "shard", scatter_dimension=0, tiled=True),
        lax.psum_scatter(small[5], "shard", scatter_dimension=0, tiled=True),
        lax.psum_scatter(small[6], "shard", scatter_dimension=0, tiled=True),
        lax.psum_scatter(small[7], "shard", scatter_dimension=0, tiled=True),
    )
    owned_qkv = contract_rows(own_columns[0], full_rows[0])
    owned_out = contract_rows(own_columns[1], full_rows[1])
    owned_up = contract_rows(own_columns[2], full_rows[2])
    owned_down = contract_rows(own_columns[3], full_rows[1])
    summed = lax.psum(
        (
            owned_qkv,
            owned_small[0],
            owned_out,
            owned_small[1],
            owned_up,
            owned_small[2],
            owned_down,
            owned_small[3],
            owned_small[4],
            owned_small[5],
            owned_small[6],
            owned_small[7],
        ),
        "replica",
    )
    return (
        block_out,
        in_grad,
        summed[0],
        summed[1],
        summed[2],
        summed[3],
        summed[4],
        summed[5],
        summed[6],
        summed[7],
        summed[8],
        summed[9],
        summed[10],
        summed[11],
    )


def solution(mesh):
    return jax.shard_map(
        body,
        mesh=mesh,
        in_specs=(
            P(("shard", "replica"), None),
            P(("shard", "replica")),
            P(("shard", "replica"), None),
            P("shard", None),
            P("shard"),
            P("shard", None),
            P("shard"),
            P("shard", None),
            P("shard"),
            P("shard", None),
            P("shard"),
            P("shard"),
            P("shard"),
            P("shard"),
            P("shard"),
        ),
        out_specs=(
            P(("shard", "replica"), None),
            P(("shard", "replica"), None),
            P("shard", None),
            P("shard"),
            P("shard", None),
            P("shard"),
            P("shard", None),
            P("shard"),
            P("shard", None),
            P("shard"),
            P("shard"),
            P("shard"),
            P("shard"),
            P("shard"),
        ),
        check_vma=False,
    )
```

profile of v0, /device:TPU:0, one launch (start us, length us, event | category | flops | bytes accessed | tf_op | source)
XLA Modules:
  0.0 2759.7 jit_solution(14352678589043947305)
XLA Ops:
  11.4 13.6 all-gather.5
  25.0 15.0 all-gather.4
  54.0 20.1 all-gather
  74.1 16.6 all-gather.2
  92.2 70.4 %all-gather.17.cloned.1.call-done = bf16[2048,2048]{1,0:T(8,128)(2,1)} async-done(((bf16[512,2048]{1,0:T(8,128)(2,1)}), bf16[2048,2048]{1,0:T(8,128)(2,1)}) %all-gather.17.cloned.1.call-update) | async-done | bytes 8388624 | tf_op jit(solution)/shard_map/all_gather | solution.py:264
  169.2 418.4 %all-gather.15.cloned.1.call-done = bf16[2048,6144]{1,0:T(8,128)(2,1)} async-done(((bf16[512,6144]{1,0:T(8,128)(2,1)}), bf16[2048,6144]{1,0:T(8,128)(2,1)}) %all-gather.15.cloned.1.call-update) | async-done | bytes 25165840 | tf_op jit(solution)/shard_map/all_gather | solution.py:262
  628.1 33.1 %all_gather.60 = bf16[8192]{0:T(1024)(128)(2,1)S(1)} all-gather(bf16[2048]{0:T(1024)(128)(2,1)S(1)} %copy-done.25), channel_id=1, replica_groups=mesh['shard'=4,'replica'=8] {'shard'}, dimensions={0}, use_global_device_ids=true | all-gather | bytes 20480 | tf_op jit(solution)/shard_map/all_gather | solution.py:267
  661.2 487.9 %all-gather.19.cloned.1.call-done = bf16[2048,8192]{1,0:T(8,128)(2,1)} async-done(((bf16[512,8192]{1,0:T(8,128)(2,1)}), bf16[2048,8192]{1,0:T(8,128)(2,1)}) %all-gather.19.cloned.1.call-update) | async-done | bytes 33554448 | tf_op jit(solution)/shard_map/all_gather | solution.py:266
  1149.1 20.1 multiply_convert_fusion
  1169.2 540.9 %all-gather.21.cloned.1.call-done = bf16[8192,2048]{1,0:T(8,128)(2,1)} async-done(((bf16[2048,2048]{1,0:T(8,128)(2,1)}), bf16[8192,2048]{1,0:T(8,128)(2,1)}) %all-gather.21.cloned.1.call-update) | async-done | bytes 33554448 | tf_op jit(solution)/shard_map/all_gather | solution.py:268
  1710.1 18.9 fusion.67
  1737.7 26.8 all-to-all-done.1
  1779.5 24.0 all-to-all-done
  1803.5 84.4 %all-gather.23.cloned.1.call-done = bf16[512,6144]{0,1:T(8,128)(2,1)} async-done(((bf16[128,6144]{0,1:T(8,128)(2,1)}), bf16[512,6144]{0,1:T(8,128)(2,1)}) %all-gather.23.cloned.1.call-update) | async-done | bytes 6291472 | tf_op jit(solution)/shard_map/all_gather | solution.py:293
  1905.9 17.3 fusion.72
  1923.2 15.5 fusion.37
  1942.6 69.0 %all-to-all-done.3 = bf16[128,4,2048]{2,0,1:T(8,128)(2,1)} async-done(((bf16[128,4,2048]{2,0,1:T(8,128)(2,1)}), bf16[128,4,2048]{2,0,1:T(8,128)(2,1)}, u32[]{:S(2)}, u32[]{:S(2)}) %all-to-all-start.3) | async-done | bytes 2097184 | tf_op jit(solution)/shard_map/all_to_all | solution.py:301
  2029.0 16.0 all-to-all-done.2
  2044.9 50.6 %all-gather.27.cloned.1.call-done = bf16[512,8192]{1,0:T(8,128)(2,1)} async-done(((bf16[128,8192]{1,0:T(8,128)(2,1)}), bf16[512,8192]{1,0:T(8,128)(2,1)}) %all-gather.27.cloned.1.call-update) | async-done | bytes 8388624 | tf_op jit(solution)/shard_map/all_gather | solution.py:295
  2095.5 14.3 fusion.75
  2141.7 15.8 fusion.7
  2162.7 24.8 all-reduce.7
  2187.5 529.5 %all-reduce.13.cloned.1.call-done = (f32[512,6144]{1,0:T(8,128)}, f32[512,2048]{1,0:T(8,128)}, f32[512,8192]{1,0:T(8,128)}, f32[2048,2048]{1,0:T(8,128)}) async-done(((f32[512,6144]{1,0:T(8,128)}, f32[512,2048]{1,0:T(8,128)}, f32[512,8192]{1,0:T(8,128)}, f32[2048,2048]{1,0:T(8,128)}), (f32[512,6144]{1,0:T(8,128)}, f32[512,2048]{1,0:T(8,128)}, f32[512,8192]{1,0:T(8,128)}, ...) | async-done | bytes 50331664 | tf_op jit(solution)/shard_map/psum | solution.py:317
  2730.7 13.9 copy.159
  (187 shorter events, 186.0 us)
Async XLA Ops:
  7.2 155.5 %all-gather.17.cloned.1.call-start = ((), (), s32[]{:S(2)}) async-start(), calls=%async_computation.5 | async-start | bytes 10485760 | tf_op jit(solution)/shard_map/all_gather | solution.py:264
  7.9 579.8 %all-gather.15.cloned.1.call-start = ((), (), s32[]{:S(2)}) async-start(), calls=%async_computation.4 | async-start | bytes 31457280 | tf_op jit(solution)/shard_map/all_gather | solution.py:262
  8.7 1140.4 %all-gather.19.cloned.1.call-start = ((), (), s32[]{:S(2)}) async-start(), calls=%async_computation.6 | async-start | bytes 41943040 | tf_op jit(solution)/shard_map/all_gather | solution.py:266
  9.4 30.6 %copy-start = (bf16[128,2048]{1,0:T(8,128)(2,1)S(1)}, bf16[128,2048]{1,0:T(8,128)(2,1)}, u32[]{:S(2)}) copy-start(bf16[128,2048]{1,0:T(8,128)(2,1)} %param.15) | copy-start | bytes 1572868
  9.4 31.1 %copy-start.30 = (bf16[512]{0:T(512)(128)(2,1)S(1)}, bf16[512]{0:T(512)(128)(2,1)}, u32[]{:S(2)}) copy-start(bf16[512]{0:T(512)(128)(2,1)} %param.27) | copy-start | bytes 3076
  9.4 44.6 %copy-start.31 = (bf16[512]{0:T(512)(128)(2,1)S(1)}, bf16[512]{0:T(512)(128)(2,1)}, u32[]{:S(2)}) copy-start(bf16[512]{0:T(512)(128)(2,1)} %param.26) | copy-start | bytes 3076
  9.5 64.6 %copy-start.26 = (bf16[1536]{0:T(1024)(128)(2,1)S(1)}, bf16[1536]{0:T(1024)(128)(2,1)}, u32[]{:S(2)}) copy-start(bf16[1536]{0:T(1024)(128)(2,1)} %param.19) | copy-start | bytes 9220
  9.5 153.2 %copy-start.9 = (bf16[128,2048]{1,0:T(8,128)(2,1)S(1)}, bf16[128,2048]{1,0:T(8,128)(2,1)}, u32[]{:S(2)}) copy-start(bf16[128,2048]{1,0:T(8,128)(2,1)} %param.17) | copy-start | bytes 1572868
  9.5 1700.6 %all-gather.21.cloned.1.call-start = ((), (), s32[]{:S(2)}) async-start(), calls=%async_computation.7 | async-start | bytes 41943040 | tf_op jit(solution)/shard_map/all_gather | solution.py:268
  10.1 1764.0 %all-gather.25.cloned.1.call-start = ((), (), s32[]{:S(2)}) async-start(), calls=%async_computation.9 | async-start | bytes 2621440 | tf_op jit(solution)/shard_map/all_gather | solution.py:294
  10.6 1877.2 %all-gather.23.cloned.1.call-start = ((), (), s32[]{:S(2)}) async-start(), calls=%async_computation.8 | async-start | bytes 7864320 | tf_op jit(solution)/shard_map/all_gather | solution.py:293
  40.2 128.7 %copy-start.21 = (f32[128]{0:T(128)}, f32[128]{0:T(128)S(1)}, u32[]{:S(2)}) copy-start(f32[128]{0:T(128)S(1)} %broadcast_multiply_fusion.4) | copy-start | bytes 1540
  40.5 128.4 %copy-start.23 = (f32[128]{0:T(128)}, f32[128]{0:T(128)S(1)}, u32[]{:S(2)}) copy-start(f32[128]{0:T(128)S(1)} %add_rsqrt_fusion) | copy-start | bytes 1540
  92.2 495.5 %copy-start.4 = (bf16[128,2048]{1,0:T(8,128)(2,1)}, bf16[128,2048]{1,0:T(8,128)(2,1)S(1)}, u32[]{:S(2)}) copy-start(bf16[128,2048]{1,0:T(8,128)(2,1)S(1)} %get-tuple-element.61) | copy-start | bytes 1572868
  92.2 1056.9 %copy-start.5 = (bf16[128,2048]{1,0:T(8,128)(2,1)}, bf16[128,2048]{1,0:T(8,128)(2,1)S(1)}, u32[]{:S(2)}) copy-start(bf16[128,2048]{1,0:T(8,128)(2,1)S(1)} %get-tuple-element.60) | copy-start | bytes 1572868
  169.2 435.0 %copy-start.7 = (bf16[128,2048]{0,1:T(8,128)(2,1)}, bf16[128,2048]{0,1:T(8,128)(2,1)S(1)}, u32[]{:S(2)}) copy-start(bf16[128,2048]{0,1:T(8,128)(2,1)S(1)} %copy.103) | copy-start | bytes 1572868
  628.0 1467.5 %all-gather.27.cloned.1.call-start = ((), (), s32[]{:S(2)}) async-start(), calls=%async_computation.10 | async-start | bytes 10485760 | tf_op jit(solution)/shard_map/all_gather | solution.py:295
  1731.7 32.8 %all-to-all-start.1 = ((bf16[128,4,512]{2,0,1:T(8,128)(2,1)}), bf16[128,4,512]{2,0,1:T(8,128)(2,1)}, u32[]{:S(2)}, u32[]{:S(2)}) async-start(bf16[128,4,512]{2,0,1:T(8,128)(2,1)} %copy.92), calls=%async_computation.1 | async-start | bytes 1048576 | tf_op jit(solution)/shard_map/all_to_all | solution.py:299
  1764.5 39.0 %all-to-all-start = ((bf16[128,4,512]{2,0,1:T(8,128)(2,1)}), bf16[128,4,512]{2,0,1:T(8,128)(2,1)}, u32[]{:S(2)}, u32[]{:S(2)}) async-start(bf16[128,4,512]{2,0,1:T(8,128)(2,1)} %bitcast.112), calls=%async_computation | async-start | bytes 1048576 | tf_op jit(solution)/shard_map/all_to_all | solution.py:298
  1901.3 110.3 %all-to-all-start.3 = ((bf16[128,4,2048]{2,0,1:T(8,128)(2,1)}), bf16[128,4,2048]{2,0,1:T(8,128)(2,1)}, u32[]{:S(2)}, u32[]{:S(2)}) async-start(bf16[128,4,2048]{2,0,1:T(8,128)(2,1)} %bitcast.96), calls=%async_computation.3 | async-start | bytes 4194304 | tf_op jit(solution)/shard_map/all_to_all | solution.py:301
  1905.8 251.6 %all-reduce.15.cloned.1.call-start = ((), (), s32[]{:S(2)}) async-start(), calls=%async_computation.12 | async-start | bytes 196608
  2011.6 33.3 %all-to-all-start.2 = ((bf16[128,4,512]{2,0,1:T(8,128)(2,1)}), bf16[128,4,512]{2,0,1:T(8,128)(2,1)}, u32[]{:S(2)}, u32[]{:S(2)}) async-start(bf16[128,4,512]{2,0,1:T(8,128)(2,1)} %bitcast.111), calls=%async_computation.2 | async-start | bytes 1048576 | tf_op jit(solution)/shard_map/all_to_all | solution.py:300
  2016.0 701.1 %all-reduce.13.cloned.1.call-start = ((), (), s32[]{:S(2)}) async-start(), calls=%async_computation.11 | async-start | bytes 100663296 | tf_op jit(solution)/shard_map/psum | solution.py:317
  2187.5 541.1 %copy-start.27 = (f32[512]{0:T(512)}, f32[512]{0:T(512)S(1)}, u32[]{:S(2)}) copy-start(f32[512]{0:T(512)S(1)} %get-tuple-element.112) | copy-start | bytes 6148
  (29 other events, 217.2 us)
Sparse Core Ops, SparseCore 0:
  9.6 153.0 all-gather.16
  164.2 423.3 all-gather.14
  589.2 559.8 all-gather.18
  1150.5 559.5 all-gather.20
  1711.5 55.0 all-gather.24
  1768.1 119.7 all-gather.22
  1890.0 205.4 all-gather.26
  2099.0 33.4 all-reduce.14
  2137.8 579.1 all-reduce.12
where the time goes:
time: 2760 us
  waiting for transfers between devices  2320 us (84%)
  matrix products  165 us (6%)
  blocking collectives  160 us (6%)
  local copies, waits for them, and re-layouts  58.2 us (2%)
    all_gather x1, waiting for transfers between devices, body(): lax.all_gather(w_down, 'shard', axis=0, tiled=True)  541 us
    psum x1, waiting for transfers between devices, body(): lax.psum((owned_qkv, owned_small[0], owned_out, owned_small[1], owned_up,...  530 us
    all_gather x1, waiting for transfers between devices, body(): lax.all_gather(w_up, 'shard', axis=0, tiled=True)  488 us
    all_gather x1, waiting for transfers between devices, body(): lax.all_gather(w_qkv, 'shard', axis=0, tiled=True)  418 us
    all_gather x1, waiting for transfers between devices, body(): lax.all_gather(mixed_low, 'shard', axis=0, tiled=True)  84.4 us
    all_gather x1, waiting for transfers between devices, body(): lax.all_gather(w_out, 'shard', axis=0, tiled=True)  70.4 us
    all_to_all x1, waiting for transfers between devices, body(): lax.all_to_all(activated, 'shard', split_axis=1, concat_axis=0, tiled=True)  69 us
    dot_general x4, matrix products, times_transpose(): lax.dot_general(left, right, (((1,), (1,)), ((), ())), preferred_element_...  57.9 us
  transfers between devices with their start and end apart: 13, of which 11 were waited for; matrix products, arithmetic and copies ran while one was open for 7% of the time, Pallas kernels for 0%

commit v1 on v0

--- a/solution.py
+++ b/solution.py
@@ -8,6 +8,32 @@
 HD = 256
 ROT = 64
 epsilon = 1e-05
+
+
+def page_enter(piece_in, dim_i):
+    piece_in = jnp.moveaxis(piece_in, 0, dim_i)
+    arr_now = piece_in.shape
+    return piece_in.reshape(
+        *arr_now[:dim_i], arr_now[dim_i] * arr_now[dim_i + 1], *arr_now[dim_i + 2 :]
+    )
+
+
+def try_all_sector(work_x, group_axis):
+    response = lax.axis_index(group_axis)
+    met_up = lax.axis_size(group_axis)
+    side_arr, raw_out = (met_up, response)
+    a_now, earlier = (work_x[None], 1)
+    while earlier < side_arr:
+        nodes = []
+        for j0 in range(side_arr):
+            nodes.append((j0, j0 ^ earlier))
+        t1 = lax.ppermute(a_now, axis_name=group_axis, perm=nodes)
+        local_out = raw_out & earlier == 0
+        block_next = jnp.where(local_out, a_now, t1)
+        block_last = jnp.where(local_out, t1, a_now)
+        a_now = jnp.concatenate([block_next, block_last])
+        earlier *= 2
+    return a_now
 
 
 def norm_forward(values, gain, shift):
@@ -258,12 +284,17 @@
     second_gain,
     second_shift,
 ):
+
+    def connect_inputs(local_x, load, in_dim):
+        then = try_all_sector(local_x, load)
+        return page_enter(then, in_dim)
+
     gathered = (
         lax.all_gather(w_qkv, "shard", axis=0, tiled=True),
         lax.all_gather(b_qkv, "shard", axis=0, tiled=True),
         lax.all_gather(w_out, "shard", axis=0, tiled=True),
         lax.all_gather(b_out, "shard", axis=0, tiled=True),
-        lax.all_gather(w_up, "shard", axis=0, tiled=True),
+        connect_inputs(w_up, "shard", in_dim=0),
         lax.all_gather(b_up, "shard", axis=0, tiled=True),
         lax.all_gather(w_down, "shard", axis=0, tiled=True),
         lax.all_gather(b_down, "shard", axis=0, tiled=True),

time: 2760 us -> 3640 us (1.32)
  blocking collectives: 160 us -> 1520 us
  waiting for transfers between devices: 2320 us -> 1780 us
  other arithmetic: 20.2 us -> 79.4 us
    all_gather x1, blocking collectives: 33.1 us -> 1390 us  [body(): lax.all_gather(b_up, 'shard', axis=0, tiled=True)]
    ppermute x0 -> x2, waiting for transfers between devices: none -> 631 us  [try_all_sector(): t1 = lax.ppermute(a_now, axis_name=group_axis, perm=nodes)]
    all_gather x1, waiting for transfers between devices: 541 us -> 0.01 us  [body(): lax.all_gather(w_down, 'shard', axis=0, tiled=True)]
    all_gather x1, waiting for transfers between devices: 488 us -> 0.01 us  [body(): lax.all_gather(w_up, 'shard', axis=0, tiled=True)]
    all_gather x1, waiting for transfers between devices: 84.4 us -> 0.02 us  [body(): lax.all_gather(mixed_low, 'shard', axis=0, tiled=True)]
    all_gather x1, waiting for transfers between devices: 50.6 us -> 0.02 us  [body(): lax.all_gather(hidden_low, 'shard', axis=0, tiled=True)]
  transfers between devices with their start and end apart: 13 -> 15, of which waited for: 11 -> 7; matrix products, arithmetic and copies ran while one was open for 7% -> 7% of each run, Pallas kernels for 0% -> 0%
where the time goes in v1:
time: 3640 us; the launch traced here: 3630 us
  waiting for transfers between devices  1780 us (49%)
  blocking collectives  1520 us (42%)
  matrix products  159 us (4%)
  other arithmetic  79.4 us (2%)
  local copies, waits for them, and re-layouts  60.3 us (2%)
    all_gather x1, blocking collectives, body(): lax.all_gather(b_up, 'shard', axis=0, tiled=True)  1390 us
    ppermute x2, waiting for transfers between devices, try_all_sector(): t1 = lax.ppermute(a_now, axis_name=group_axis, perm=nodes)  631 us
    psum x1, waiting for transfers between devices, body(): lax.psum((owned_qkv, owned_small[0], owned_out, owned_small[1], owned_up,...  529 us
    all_gather x1, waiting for transfers between devices, body(): lax.all_gather(w_qkv, 'shard', axis=0, tiled=True)  418 us
    all_to_all x1, waiting for transfers between devices, body(): lax.all_to_all(activated, 'shard', split_axis=1, concat_axis=0, tiled=True)  98.5 us
  transfers between devices with their start and end apart: 15, of which 7 were waited for; matrix products, arithmetic and copies ran while one was open for 7% of the time, Pallas kernels for 0%

profile of v1, /device:TPU:0, one launch (start us, length us, event | category | flops | bytes accessed | tf_op | source)
XLA Modules:
  0.0 3632.1 jit_solution(17133252221766404275)
XLA Ops:
  10.8 13.6 all-gather.5
  24.4 15.7 all-gather.4
  40.7 13.3 all-gather.1
  54.0 20.0 all-gather
  74.1 16.6 all-gather.2
  92.2 70.4 %all-gather.17.cloned.1.call-done = bf16[2048,2048]{1,0:T(8,128)(2,1)} async-done(((bf16[512,2048]{1,0:T(8,128)(2,1)}), bf16[2048,2048]{1,0:T(8,128)(2,1)}) %all-gather.17.cloned.1.call-update) | async-done | bytes 8388624 | tf_op jit(solution)/shard_map/all_gather | solution.py:295
  169.2 418.4 %all-gather.15.cloned.1.call-done = bf16[2048,6144]{1,0:T(8,128)(2,1)} async-done(((bf16[512,6144]{1,0:T(8,128)(2,1)}), bf16[2048,6144]{1,0:T(8,128)(2,1)}) %all-gather.15.cloned.1.call-update) | async-done | bytes 25165840 | tf_op jit(solution)/shard_map/all_gather | solution.py:293
  587.6 12.8 convolution_add_fusion.1
  629.1 631.3 %collective-permute-done = bf16[1,512,8192]{2,1,0:T(8,128)(2,1)} collective-permute-done((bf16[1,512,8192]{2,1,0:T(8,128)(2,1)}, bf16[1,512,8192]{2,1,0:T(8,128)(2,1)}, u32[]{:S(2)}, u32[]{:S(2)}) %collective-permute-start) | collective-permute-done | bytes 8388640 | tf_op jit(solution)/shard_map/ppermute | solution.py:30
  1278.1 1388.1 %all_gather.58 = bf16[8192]{0:T(1024)(128)(2,1)S(1)} all-gather(bf16[2048]{0:T(1024)(128)(2,1)S(1)} %copy-done.31), channel_id=1, replica_groups=mesh['shard'=4,'replica'=8] {'shard'}, dimensions={0}, use_global_device_ids=true | all-gather | bytes 20480 | tf_op jit(solution)/shard_map/all_gather | solution.py:298
  2666.2 22.6 broadcast_select_fusion.1
  2688.8 22.9 pad_maximum_fusion
  2711.7 15.3 multiply_convert_fusion
  2727.0 18.9 fusion.67
  2755.4 98.5 %all-to-all-done.3 = bf16[128,4,2048]{2,0,1:T(8,128)(2,1)} async-done(((bf16[128,4,2048]{2,0,1:T(8,128)(2,1)}), bf16[128,4,2048]{2,0,1:T(8,128)(2,1)}, u32[]{:S(2)}, u32[]{:S(2)}) %all-to-all-start.3) | async-done | bytes 2097184 | tf_op jit(solution)/shard_map/all_to_all | solution.py:332
  2861.8 22.3 all-to-all-done.1
  2888.5 13.1 fusion.76
  2930.6 17.6 fusion.72
  2948.2 15.4 fusion.37
  2967.6 14.3 fusion.75
  3014.2 15.6 fusion.7
  3035.0 24.8 all-reduce.7
  3059.9 529.3 %all-reduce.13.cloned.1.call-done = (f32[512,6144]{1,0:T(8,128)}, f32[512,2048]{1,0:T(8,128)}, f32[512,8192]{1,0:T(8,128)}, f32[2048,2048]{1,0:T(8,128)}) async-done(((f32[512,6144]{1,0:T(8,128)}, f32[512,2048]{1,0:T(8,128)}, f32[512,8192]{1,0:T(8,128)}, f32[2048,2048]{1,0:T(8,128)}), (f32[512,6144]{1,0:T(8,128)}, f32[512,2048]{1,0:T(8,128)}, f32[512,8192]{1,0:T(8,128)}, ...) | async-done | bytes 50331664 | tf_op jit(solution)/shard_map/psum | solution.py:348
  3602.9 13.9 copy.159
  (207 shorter events, 170.1 us)
Async XLA Ops:
  7.2 155.4 %all-gather.17.cloned.1.call-start = ((), (), s32[]{:S(2)}) async-start(), calls=%async_computation.5 | async-start | bytes 10485760 | tf_op jit(solution)/shard_map/all_gather | solution.py:295
  8.0 579.7 %all-gather.15.cloned.1.call-start = ((), (), s32[]{:S(2)}) async-start(), calls=%async_computation.4 | async-start | bytes 31457280 | tf_op jit(solution)/shard_map/all_gather | solution.py:293
  8.7 45.3 %copy-start.37 = (bf16[512]{0:T(512)(128)(2,1)S(1)}, bf16[512]{0:T(512)(128)(2,1)}, u32[]{:S(2)}) copy-start(bf16[512]{0:T(512)(128)(2,1)} %param.26) | copy-start | bytes 3076
  8.7 65.4 %copy-start.32 = (bf16[1536]{0:T(1024)(128)(2,1)S(1)}, bf16[1536]{0:T(1024)(128)(2,1)}, u32[]{:S(2)}) copy-start(bf16[1536]{0:T(1024)(128)(2,1)} %param.19) | copy-start | bytes 9220
  8.7 153.9 %copy-start.14 = (bf16[128,2048]{1,0:T(8,128)(2,1)S(1)}, bf16[128,2048]{1,0:T(8,128)(2,1)}, u32[]{:S(2)}) copy-start(bf16[128,2048]{1,0:T(8,128)(2,1)} %param.17) | copy-start | bytes 1572868
  8.7 2718.3 %all-gather.19.cloned.1.call-start = ((), (), s32[]{:S(2)}) async-start(), calls=%async_computation.6 | async-start | bytes 41943040 | tf_op jit(solution)/shard_map/all_gather | solution.py:299
  9.5 2879.0 %all-gather.25.cloned.1.call-start = ((), (), s32[]{:S(2)}) async-start(), calls=%async_computation.9 | async-start | bytes 2621440 | tf_op jit(solution)/shard_map/all_gather | solution.py:325
  10.1 2909.3 %all-gather.23.cloned.1.call-start = ((), (), s32[]{:S(2)}) async-start(), calls=%async_computation.8 | async-start | bytes 7864320 | tf_op jit(solution)/shard_map/all_gather | solution.py:324
  40.4 128.8 %copy-start.27 = (f32[128]{0:T(128)}, f32[128]{0:T(128)S(1)}, u32[]{:S(2)}) copy-start(f32[128]{0:T(128)S(1)} %broadcast_multiply_fusion.4) | copy-start | bytes 1540
  40.7 559.8 %copy-start.29 = (f32[128]{0:T(128)}, f32[128]{0:T(128)S(1)}, u32[]{:S(2)}) copy-start(f32[128]{0:T(128)S(1)} %add_rsqrt_fusion) | copy-start | bytes 1540
  92.2 508.2 %copy-start.9 = (bf16[128,2048]{1,0:T(8,128)(2,1)}, bf16[128,2048]{1,0:T(8,128)(2,1)S(1)}, u32[]{:S(2)}) copy-start(bf16[128,2048]{1,0:T(8,128)(2,1)S(1)} %get-tuple-element.65) | copy-start | bytes 1572868
  92.2 2619.5 %copy-start.10 = (bf16[128,2048]{1,0:T(8,128)(2,1)}, bf16[128,2048]{1,0:T(8,128)(2,1)S(1)}, u32[]{:S(2)}) copy-start(bf16[128,2048]{1,0:T(8,128)(2,1)S(1)} %get-tuple-element.64) | copy-start | bytes 1572868
  169.2 435.5 %copy-start.13 = (bf16[128,2048]{0,1:T(8,128)(2,1)}, bf16[128,2048]{0,1:T(8,128)(2,1)S(1)}, u32[]{:S(2)}) copy-start(bf16[128,2048]{0,1:T(8,128)(2,1)S(1)} %copy.103) | copy-start | bytes 1572868
  628.4 2302.2 %all-gather.21.cloned.1.call-start = ((), (), s32[]{:S(2)}) async-start(), calls=%async_computation.7 | async-start | bytes 41943040 | tf_op jit(solution)/shard_map/all_gather | solution.py:312
  628.9 2338.7 %all-gather.27.cloned.1.call-start = ((), (), s32[]{:S(2)}) async-start(), calls=%async_computation.10 | async-start | bytes 10485760 | tf_op jit(solution)/shard_map/all_gather | solution.py:326
  629.0 631.4 %collective-permute-start = (bf16[1,512,8192]{2,1,0:T(8,128)(2,1)}, bf16[1,512,8192]{2,1,0:T(8,128)(2,1)}, u32[]{:S(2)}, u32[]{:S(2)}) collective-permute-start(bf16[1,512,8192]{2,1,0:T(8,128)(2,1)} %bitcast.92), channel_id=1, source_target_pairs={{0,8},{8,0},{16,24},{24,16},{1,9},{9,1},{17,25},{25,17},{2,10},{10... | collective-permute-start | bytes 25165832 | tf_op jit(solution)/shard_map/ppermute | solution.py:30
  1278.1 1388.1 %collective-permute-start.1 = (bf16[2,512,8192]{2,1,0:T(8,128)(2,1)}, bf16[2,512,8192]{2,1,0:T(8,128)(2,1)}, u32[]{:S(2)}, u32[]{:S(2)}) collective-permute-start(bf16[2,512,8192]{2,1,0:T(8,128)(2,1)} %pad_maximum_fusion.1), channel_id=1, source_target_pairs={{0,16},{8,24},{16,0},{24,8},{1,17},{9,25},{17,1},{25,9},{2,18},{10... | collective-permute-start | bytes 50331656 | tf_op jit(solution)/shard_map/ppermute | solution.py:30
  2747.4 106.4 %all-to-all-start.3 = ((bf16[128,4,2048]{2,0,1:T(8,128)(2,1)}), bf16[128,4,2048]{2,0,1:T(8,128)(2,1)}, u32[]{:S(2)}, u32[]{:S(2)}) async-start(bf16[128,4,2048]{2,0,1:T(8,128)(2,1)} %bitcast.102), calls=%async_computation.3 | async-start | bytes 4194304 | tf_op jit(solution)/shard_map/all_to_all | solution.py:332
  2853.8 30.2 all-to-all-start.1
  2884.1 31.0 all-to-all-start
  2915.1 52.5 %all-to-all-start.2 = ((bf16[128,4,512]{2,0,1:T(8,128)(2,1)}), bf16[128,4,512]{2,0,1:T(8,128)(2,1)}, u32[]{:S(2)}, u32[]{:S(2)}) async-start(bf16[128,4,512]{2,0,1:T(8,128)(2,1)} %bitcast.117), calls=%async_computation.2 | async-start | bytes 1048576 | tf_op jit(solution)/shard_map/all_to_all | solution.py:331
  2919.3 110.5 %all-reduce.15.cloned.1.call-start = ((), (), s32[]{:S(2)}) async-start(), calls=%async_computation.12 | async-start | bytes 196608
  2967.5 621.7 %all-reduce.13.cloned.1.call-start = ((), (), s32[]{:S(2)}) async-start(), calls=%async_computation.11 | async-start | bytes 100663296 | tf_op jit(solution)/shard_map/psum | solution.py:348
  3059.9 540.9 %copy-start.33 = (f32[512]{0:T(512)}, f32[512]{0:T(512)S(1)}, u32[]{:S(2)}) copy-start(f32[512]{0:T(512)S(1)} %get-tuple-element.116) | copy-start | bytes 6148
  (37 other events, 375.1 us)
Sparse Core Ops, SparseCore 0:
  9.6 153.0 all-gather.16
  164.2 423.3 all-gather.14
  589.2 780.0 all-gather.18
  1370.7 367.7 all-gather.24
  1739.9 163.5 all-gather.22
  1904.9 793.4 all-gather.20
  2746.1 220.7 all-gather.26
  2970.3 34.1 all-reduce.14
  3010.0 579.1 all-reduce.12
